TPU v7x, 32 devices: a whole 2x2x4 slice. The times are simulated.
32 devices in a mesh: row: 8 (over y, x, core), col: 4 (over z).
Axes of the slice: x: 2, y: 2, z: 4, core: 2. Of those that a mesh axis runs over, the one named last changes fastest.
Arguments:
- pair_factors: float32 [12288, 1024], P(('row', 'col')), may hold values from -0.09375 to 0.09375
- k_prev: float32 [12288, 12288], P('row', 'col'), as said below
- energies: float32 [12288], P('row'), may hold values from 0.3 to 2
Outputs:
- casida: float32 [12288, 12288], P('row', 'col')
- vectors: float32 [12288, 8], P('row')
- images: float32 [12288, 8], P('row')
- tridiagonal: float32 [2, 8], replicated
Inputs may be any that keep to these rules, and one draw needn't show every extreme that they name: k_prev is exactly symmetric.
All inputs are finite; a program needn't handle non-finite values.
Results may differ from a plain program's by a relative error of at most 0.0003.
Values sent between devices are 32-bit elements; how exact they have to be, the bound alone decides.
No kernel may reach another device: no remote copies, remote signals or barrier semaphores. Data moves between devices by JAX's collectives and lax.ppermute only.
A program may use at most 128 MiB of HBM per device.

v0:
```python
import jax
import jax.numpy as jnp
from jax import lax
from jax.sharding import PartitionSpec as P

N = 12288
PANEL_W = 512
PC = 8


def from_root(value, axis, root):
    mine = lax.axis_index(axis) == root
    return lax.psum(jnp.where(mine, value, jnp.zeros_like(value)), axis)


def shards(pair_factors, k_prev, energies):
    rows_here, cols_here = k_prev.shape
    per_col = lax.axis_size("row") // lax.axis_size("col")
    row_index = lax.axis_index("row")
    col_index = lax.axis_index("col")
    total = jnp.zeros((rows_here, cols_here), jnp.float32)
    aux_here = pair_factors.shape[1]
    width = PANEL_W
    for start_at in range(0, aux_here, width):
        stop_at = min(start_at + width, aux_here)
        piece = pair_factors[:, start_at:stop_at]
        left_rows = lax.all_gather(piece, "col", axis=0, tiled=True)
        right_parts = []
        for offset in range(per_col):
            right_parts.append(from_root(left_rows, "row", per_col * col_index + offset))
        right_rows = jnp.concatenate(right_parts, axis=0)
        total = total + lax.dot_general(
            left_rows,
            right_rows,
            (((1,), (1,)), ((), ())),
            precision=lax.Precision.HIGHEST,
            preferred_element_type=jnp.float32,
        )
    global_rows = row_index * rows_here + jnp.arange(rows_here, dtype=jnp.int32)
    global_cols = col_index * cols_here + jnp.arange(cols_here, dtype=jnp.int32)
    on_diagonal = global_rows[:, None] == global_cols[None, :]
    casida = 4.0 * (k_prev + total) + jnp.where(on_diagonal, energies[:, None], 0.0)
    col_ids = jnp.arange(PC, dtype=jnp.int32)
    scale = jnp.sqrt(jnp.float32(N))
    diag_list = []
    sub_list = []
    spread = from_root(casida[:, :PC], "col", 0)
    panel = lax.all_gather(spread, "row", axis=0, tiled=True)
    total_rows = panel.shape[0]
    all_rows = jnp.arange(total_rows, dtype=jnp.int32)
    upper_full = jnp.zeros((total_rows, PC), jnp.float32)
    lower_full = jnp.zeros((total_rows, PC), jnp.float32)
    for column_at in range(PC):
        column = (
            panel[:, column_at]
            - jnp.dot(upper_full, lower_full[column_at], precision=lax.Precision.HIGHEST)
            - jnp.dot(lower_full, upper_full[column_at], precision=lax.Precision.HIGHEST)
        )
        diag_list.append(column[column_at])
        below = jnp.where(all_rows > column_at, column, 0.0)
        lead = column[column_at + 1]
        sigma = jnp.sum(below * below)
        root = jnp.sqrt(sigma)
        alpha = jnp.where(lead >= 0, -root, root)
        length = jnp.sqrt(jnp.maximum(2.0 * (sigma + jnp.abs(lead) * root), 1.0))
        unit = (below - alpha * (all_rows == column_at + 1).astype(jnp.float32)) / length
        unit_cols = lax.dynamic_slice_in_dim(unit, col_index * cols_here, cols_here, 0)
        partial_rows = jnp.dot(casida, unit_cols, precision=lax.Precision.HIGHEST)
        placed = lax.dynamic_update_slice_in_dim(
            jnp.zeros((total_rows,), jnp.float32), partial_rows, row_index * rows_here, 0
        )
        image = lax.psum(placed, ("row", "col"))
        image = image - jnp.dot(
            upper_full,
            jnp.dot(lower_full.T, unit, precision=lax.Precision.HIGHEST),
            precision=lax.Precision.HIGHEST,
        )
        image = image - jnp.dot(
            lower_full,
            jnp.dot(upper_full.T, unit, precision=lax.Precision.HIGHEST),
            precision=lax.Precision.HIGHEST,
        )
        image = 2.0 * image
        partner = image - jnp.sum(image * unit) * unit
        pick = (col_ids == column_at).astype(jnp.float32)[None, :]
        upper_full = upper_full + unit[:, None] * pick
        lower_full = lower_full + partner[:, None] * pick
        sub_list.append(alpha)
    upper = lax.dynamic_slice_in_dim(upper_full, row_index * rows_here, rows_here, 0)
    lower = lax.dynamic_slice_in_dim(lower_full, row_index * rows_here, rows_here, 0)
    tridiagonal = jnp.stack([jnp.stack(diag_list), jnp.stack(sub_list)])
    return (casida, scale * upper, scale * lower, tridiagonal)


def solution(mesh):
    in_specs = (P(("row", "col"), None), P("row", "col"), P("row"))
    out_specs = (P("row", "col"), P("row", None), P("row", None), P())
    return jax.shard_map(shards, mesh=mesh, in_specs=in_specs, out_specs=out_specs, check_vma=False)
```

profile of v0, /device:TPU:0, one launch (start us, length us, event | category | flops | bytes accessed | tf_op | source)
XLA Modules:
  0.0 965.6 jit_solution(18281307544850483089)
XLA Ops:
  7.2 2.6 fusion.234
  10.7 65.6 %all-gather.5.cloned.1.call-done = f32[1536,512]{1,0:T(8,128)} async-done(((f32[384,512]{1,0:T(8,128)}), f32[1536,512]{1,0:T(8,128)}) %all-gather.5.cloned.1.call-update) | async-done | bytes 3145744 | tf_op jit(solution)/shard_map/all_gather | solution.py:27
  76.3 5.6 broadcast_select_fusion.1
  81.9 58.1 %all-gather.3.cloned.1.call-done = f32[1536,512]{1,0:T(8,128)} async-done(((f32[384,512]{1,0:T(8,128)}), f32[1536,512]{1,0:T(8,128)}) %all-gather.3.cloned.1.call-update) | async-done | bytes 3145744 | tf_op jit(solution)/shard_map/all_gather | solution.py:27
  140.0 5.6 broadcast_select_fusion.3
  146.3 18.8 %copy.9 = f32[1536,3072]{0,1:T(8,128)} copy(f32[1536,3072]{1,0:T(8,128)} %param.4) | data formatting | bytes 37748736 | tf_op args[1]
  165.1 151.2 %all-reduce.3.cloned.1.call-done = (f32[1536,512]{1,0:T(8,128)}, f32[1536,512]{1,0:T(8,128)}, f32[1536,512]{1,0:T(8,128)}, f32[1536,512]{1,0:T(8,128)}) async-done(((f32[1536,512]{1,0:T(8,128)}, f32[1536,512]{1,0:T(8,128)}, f32[1536,512]{1,0:T(8,128)}, f32[1536,512]{1,0:T(8,128)}), (f32[1536,512]{1,0:T(8,128)}, f32[1536,512]{1,0:T(8,128)}, f32[1536,512]{1,0:T(8,128)}, ...) | async-done | bytes 12582928 | tf_op jit(solution)/shard_map/psum | solution.py:13
  316.4 34.6 %fusion.2 = f32[3072,1536]{1,0:T(8,128)} fusion(f32[1536,512]{1,0:T(8,128)S(1)} %copy-done.1, f32[1536,512]{1,0:T(8,128)} %get-tuple-element.12, f32[1536,512]{1,0:T(8,128)} %get-tuple-element.13), kind=kOutput, calls=%fused_computation.3 | convolution fusion | flops 28992602112 | bytes 28311552 | tf_op jit(solution)/shard_map/dot_general | solution.py:32
  351.0 39.2 %fusion.1 = f32[1536,3072]{0,1:T(8,128)S(1)} fusion(f32[1536,3072]{0,1:T(8,128)} %copy.9, f32[3072,1536]{1,0:T(8,128)} %fusion.2, f32[1536,512]{1,0:T(8,128)} %all-gather.5.cloned.1.call-done, f32[1536]{0:T(1024)S(1)} %copy-done.2, s32[1536]{0:T(1024)S(1)} %iota_add_fusion.1, s32[3072]{0:T(1024)S(1)} %iota_add_fusion, f32[1536,512]{1,0:T(8,128)} %get-tuple-element.14, ...), kind=kOutput, calls=%fused_computation.2 | convolution fusion | flops 29020913664 | bytes 66084864 | tf_op jit(solution)/shard_map/dot_general | solution.py:32
  390.2 6.5 copy-done
  396.7 19.5 %psum.95 = f32[1536,8]{0,1:T(8,128)S(1)} all-reduce(f32[1536,8]{0,1:T(8,128)S(1)} %slice_select_fusion), channel_id=1, replica_groups=mesh['row'=8,'col'=4] {'col'}, use_global_device_ids=true, to_apply=%region_4.5 | all-reduce | flops 12288 | bytes 98304 | tf_op jit(solution)/shard_map/psum | solution.py:13
  416.2 9.5 all_gather.11
  430.6 12.9 %convolution_reduce_fusion.7 = f32[1536]{0:T(1024)S(1)} fusion(f32[1536,3072]{0,1:T(8,128)} %copy-done, f32[3072,1]{0,1:T(1,128)S(1)} %bitcast.304), kind=kOutput, calls=%fused_computation.21 | convolution fusion | flops 56623104 | bytes 18892800 | tf_op jit(solution)/shard_map/dot_general | solution.py:68
  443.8 38.0 %psum.96 = f32[12288]{0:T(1024)S(1)} all-reduce(f32[12288]{0:T(1024)S(1)} %dynamic_update_slice.24), channel_id=1, replica_groups=mesh['row'=8,'col'=4] {'row','col'}, use_global_device_ids=true, to_apply=%region_6.7 | all-reduce | flops 12288 | bytes 98304 | tf_op jit(solution)/shard_map/psum | solution.py:72
  481.8 1.6 fusion.12
  493.4 12.9 %convolution_reduce_fusion.6 = f32[1536]{0:T(1024)S(1)} fusion(f32[1536,3072]{0,1:T(8,128)} %copy-done, f32[3072,1]{0,1:T(1,128)S(1)} %bitcast.298), kind=kOutput, calls=%fused_computation.20 | convolution fusion | flops 56623104 | bytes 18892800 | tf_op jit(solution)/shard_map/dot_general | solution.py:68
  506.6 41.5 %psum.97 = f32[12288]{0:T(1024)S(1)} all-reduce(f32[12288]{0:T(1024)S(1)} %dynamic_update_slice.25), channel_id=1, replica_groups=mesh['row'=8,'col'=4] {'row','col'}, use_global_device_ids=true, to_apply=%region_9.10 | all-reduce | flops 12288 | bytes 98304 | tf_op jit(solution)/shard_map/psum | solution.py:72
  558.1 12.9 %convolution_reduce_fusion.5 = f32[1536]{0:T(1024)S(1)} fusion(f32[1536,3072]{0,1:T(8,128)} %copy-done, f32[3072,1]{0,1:T(1,128)S(1)} %bitcast.299), kind=kOutput, calls=%fused_computation.19 | convolution fusion | flops 56623104 | bytes 18892800 | tf_op jit(solution)/shard_map/dot_general | solution.py:68
  571.3 39.9 %psum.98 = f32[12288]{0:T(1024)S(1)} all-reduce(f32[12288]{0:T(1024)S(1)} %dynamic_update_slice.26), channel_id=1, replica_groups=mesh['row'=8,'col'=4] {'row','col'}, use_global_device_ids=true, to_apply=%region_12.13 | all-reduce | flops 12288 | bytes 98304 | tf_op jit(solution)/shard_map/psum | solution.py:72
  621.3 12.9 %convolution_reduce_fusion.4 = f32[1536]{0:T(1024)S(1)} fusion(f32[1536,3072]{0,1:T(8,128)} %copy-done, f32[3072,1]{0,1:T(1,128)S(1)} %bitcast.300), kind=kOutput, calls=%fused_computation.18 | convolution fusion | flops 56623104 | bytes 18892800 | tf_op jit(solution)/shard_map/dot_general | solution.py:68
  634.5 41.6 %psum.99 = f32[12288]{0:T(1024)S(1)} all-reduce(f32[12288]{0:T(1024)S(1)} %dynamic_update_slice.27), channel_id=1, replica_groups=mesh['row'=8,'col'=4] {'row','col'}, use_global_device_ids=true, to_apply=%region_15.16 | all-reduce | flops 12288 | bytes 98304 | tf_op jit(solution)/shard_map/psum | solution.py:72
  686.5 12.9 %convolution_reduce_fusion.3 = f32[1536]{0:T(1024)S(1)} fusion(f32[1536,3072]{0,1:T(8,128)} %copy-done, f32[3072,1]{0,1:T(1,128)S(1)} %bitcast.301), kind=kOutput, calls=%fused_computation.17 | convolution fusion | flops 56623104 | bytes 18892800 | tf_op jit(solution)/shard_map/dot_general | solution.py:68
  699.7 40.0 %psum.100 = f32[12288]{0:T(1024)S(1)} all-reduce(f32[12288]{0:T(1024)S(1)} %dynamic_update_slice.28), channel_id=1, replica_groups=mesh['row'=8,'col'=4] {'row','col'}, use_global_device_ids=true, to_apply=%region_18.19 | all-reduce | flops 12288 | bytes 98304 | tf_op jit(solution)/shard_map/psum | solution.py:72
  750.0 12.9 %convolution_reduce_fusion.2 = f32[1536]{0:T(1024)S(1)} fusion(f32[1536,3072]{0,1:T(8,128)} %copy-done, f32[3072,1]{0,1:T(1,128)S(1)} %bitcast.302), kind=kOutput, calls=%fused_computation.16 | convolution fusion | flops 56623104 | bytes 18892800 | tf_op jit(solution)/shard_map/dot_general | solution.py:68
  763.3 41.2 %psum.101 = f32[12288]{0:T(1024)S(1)} all-reduce(f32[12288]{0:T(1024)S(1)} %dynamic_update_slice.29), channel_id=1, replica_groups=mesh['row'=8,'col'=4] {'row','col'}, use_global_device_ids=true, to_apply=%region_21.22 | all-reduce | flops 12288 | bytes 98304 | tf_op jit(solution)/shard_map/psum | solution.py:72
  814.5 12.9 %convolution_reduce_fusion.1 = f32[1536]{0:T(1024)S(1)} fusion(f32[1536,3072]{0,1:T(8,128)} %copy-done, f32[3072,1]{0,1:T(1,128)S(1)} %bitcast.303), kind=kOutput, calls=%fused_computation.15 | convolution fusion | flops 56623104 | bytes 18892800 | tf_op jit(solution)/shard_map/dot_general | solution.py:68
  827.7 40.0 %psum.102 = f32[12288]{0:T(1024)S(1)} all-reduce(f32[12288]{0:T(1024)S(1)} %dynamic_update_slice.30), channel_id=1, replica_groups=mesh['row'=8,'col'=4] {'row','col'}, use_global_device_ids=true, to_apply=%region_24.25 | all-reduce | flops 12288 | bytes 98304 | tf_op jit(solution)/shard_map/psum | solution.py:72
  875.9 1.1 convolution_bitcast_fusion
  877.0 18.6 %copy.10 = f32[1536,3072]{1,0:T(8,128)} copy(f32[1536,3072]{0,1:T(8,128)} %copy-done) | data formatting | bytes 37748736
  896.1 12.9 %convolution_reduce_fusion = f32[1536]{0:T(1024)S(1)} fusion(f32[1536,3072]{0,1:T(8,128)} %copy-done, f32[3072,1]{0,1:T(1,128)S(1)} %bitcast.297), kind=kOutput, calls=%fused_computation.14 | convolution fusion | flops 56623104 | bytes 18892800 | tf_op jit(solution)/shard_map/dot_general | solution.py:68
  909.3 41.0 %psum.103 = f32[12288]{0:T(1024)S(1)} all-reduce(f32[12288]{0:T(1024)S(1)} %dynamic_update_slice.31), channel_id=1, replica_groups=mesh['row'=8,'col'=4] {'row','col'}, use_global_device_ids=true, to_apply=%region_27.28 | all-reduce | flops 12288 | bytes 98304 | tf_op jit(solution)/shard_map/psum | solution.py:72
  952.3 5.1 stack.39
  (156 shorter events, 60.5 us)
Async XLA Ops:
  7.2 69.2 %all-gather.5.cloned.1.call-start = ((), (), s32[]{:S(2)}) async-start(), calls=%async_computation.1 | async-start | bytes 3932160 | tf_op jit(solution)/shard_map/all_gather | solution.py:27
  9.9 130.1 %all-gather.3.cloned.1.call-start = ((), (), s32[]{:S(2)}) async-start(), calls=%async_computation | async-start | bytes 3932160 | tf_op jit(solution)/shard_map/all_gather | solution.py:27
  10.6 305.7 %all-reduce.3.cloned.1.call-start = ((), (), s32[]{:S(2)}) async-start(), calls=%async_computation.2 | async-start | bytes 25165824 | tf_op jit(solution)/shard_map/psum | solution.py:13
  146.3 170.1 %copy-start.1 = (f32[1536,512]{1,0:T(8,128)S(1)}, f32[1536,512]{1,0:T(8,128)}, u32[]{:S(2)}) copy-start(f32[1536,512]{1,0:T(8,128)} %all-gather.3.cloned.1.call-done) | copy-start | bytes 9437188
  165.0 185.9 %copy-start.2 = (f32[1536]{0:T(1024)S(1)}, f32[1536]{0:T(1024)}, u32[]{:S(2)}) copy-start(f32[1536]{0:T(1024)} %param.5) | copy-start | bytes 18436
  390.2 6.5 copy-start
Sparse Core Ops, SparseCore 0:
  10.1 66.1 all-gather.4
  77.9 62.0 all-gather.2
  145.7 170.6 all-reduce.2
where the time goes:
time: 974 us; the launch traced here: 966 us
  blocking collectives  352 us (36%)
  waiting for transfers between devices  276 us (28%)
  matrix products  208 us (21%)
  local copies, waits for them, and re-layouts  63.6 us (7%)
  between operations  35.8 us (4%)
  other arithmetic  30 us (3%)
    psum x8, blocking collectives, shards(): image = lax.psum(placed, ('row', 'col'))  323 us
    psum x1, waiting for transfers between devices, from_root(): return lax.psum(jnp.where(mine, value, jnp.zeros_like(value)), axis)  151 us
    all_gather x2, waiting for transfers between devices, shards(): left_rows = lax.all_gather(piece, 'col', axis=0, tiled=True)  124 us
    dot_general x8, matrix products, shards(): partial_rows = jnp.dot(casida, unit_cols, precision=lax.Precision.HIGHEST)  103 us
    dot_general x2, matrix products, shards(): lax.dot_general(left_rows, right_rows, (((1,), (1,)), ((), ())), precisio...  73.9 us
    unnamed x8, local copies, waits for them, and re-layouts  43.9 us
  transfers between devices with their start and end apart: 3, of which 3 were waited for; matrix products, arithmetic and copies ran while one was open for 3% of the time, Pallas kernels for 0%

commit v1 on v0

--- a/solution.py
+++ b/solution.py
@@ -69,7 +69,7 @@
         placed = lax.dynamic_update_slice_in_dim(
             jnp.zeros((total_rows,), jnp.float32), partial_rows, row_index * rows_here, 0
         )
-        image = lax.psum(placed, ("row", "col"))
+        image = jnp.sum(lax.all_gather(placed, ("row", "col")), axis=0)
         image = image - jnp.dot(
             upper_full,
             jnp.dot(lower_full.T, unit, precision=lax.Precision.HIGHEST),

time: 974 us -> 1060 us (1.088)
  waiting for transfers between devices: 276 us -> 656 us
  blocking collectives: 352 us -> 29 us
  other arithmetic: 30 us -> 49.4 us
    all_gather x0 -> x8, waiting for transfers between devices: none -> 380 us  [shards(): image = jnp.sum(lax.all_gather(placed, ('row', 'col')), axis=0)]
    psum x8 -> x0, blocking collectives: 323 us -> none  [shards(): image = lax.psum(placed, ('row', 'col'))]
    reduce_sum x0 -> x8, other arithmetic: none -> 19.5 us  [shards(): image = jnp.sum(lax.all_gather(placed, ('row', 'col')), axis=0)]
    unnamed x8 -> x32, local copies, waits for them, and re-layouts: 43.9 us -> 49.1 us
  transfers between devices with their start and end apart: 3 -> 11, of which waited for: 3 -> 11; matrix products, arithmetic and copies ran while one was open for 3% -> 7% of each run, Pallas kernels for 0% -> 0%
where the time goes in v1:
time: 1060 us; the launch traced here: 1050 us
  waiting for transfers between devices  656 us (62%)
  matrix products  208 us (20%)
  local copies, waits for them, and re-layouts  65.9 us (6%)
  other arithmetic  49.4 us (5%)
  between operations  36.5 us (3%)
  blocking collectives  29 us (3%)
    all_gather x8, waiting for transfers between devices, shards(): image = jnp.sum(lax.all_gather(placed, ('row', 'col')), axis=0)  380 us
    psum x1, waiting for transfers between devices, from_root(): return lax.psum(jnp.where(mine, value, jnp.zeros_like(value)), axis)  151 us
    all_gather x2, waiting for transfers between devices, shards(): left_rows = lax.all_gather(piece, 'col', axis=0, tiled=True)  124 us
    dot_general x8, matrix products, shards(): partial_rows = jnp.dot(casida, unit_cols, precision=lax.Precision.HIGHEST)  103 us
    dot_general x2, matrix products, shards(): lax.dot_general(left_rows, right_rows, (((1,), (1,)), ((), ())), precisio...  73.9 us
    unnamed x32, local copies, waits for them, and re-layouts  49.1 us
  transfers between devices with their start and end apart: 11, of which 11 were waited for; matrix products, arithmetic and copies ran while one was open for 7% of the time, Pallas kernels for 0%

profile of v1, /device:TPU:0, one launch (start us, length us, event | category | flops | bytes accessed | tf_op | source)
XLA Modules:
  0.0 1047.5 jit_solution(3364528772317648115)
XLA Ops:
  7.2 2.6 fusion.242
  10.7 65.6 %all-gather.21.cloned.1.call-done = f32[1536,512]{1,0:T(8,128)} async-done(((f32[384,512]{1,0:T(8,128)}), f32[1536,512]{1,0:T(8,128)}) %all-gather.21.cloned.1.call-update) | async-done | bytes 3145744 | tf_op jit(solution)/shard_map/all_gather | solution.py:27
  76.3 5.6 broadcast_select_fusion.1
  81.9 58.1 %all-gather.19.cloned.1.call-done = f32[1536,512]{1,0:T(8,128)} async-done(((f32[384,512]{1,0:T(8,128)}), f32[1536,512]{1,0:T(8,128)}) %all-gather.19.cloned.1.call-update) | async-done | bytes 3145744 | tf_op jit(solution)/shard_map/all_gather | solution.py:27
  140.0 5.6 broadcast_select_fusion.3
  146.3 18.8 %copy.11 = f32[1536,3072]{0,1:T(8,128)} copy(f32[1536,3072]{1,0:T(8,128)} %param.4) | data formatting | bytes 37748736 | tf_op args[1]
  165.1 151.3 %all-reduce.3.cloned.1.call-done = (f32[1536,512]{1,0:T(8,128)}, f32[1536,512]{1,0:T(8,128)}, f32[1536,512]{1,0:T(8,128)}, f32[1536,512]{1,0:T(8,128)}) async-done(((f32[1536,512]{1,0:T(8,128)}, f32[1536,512]{1,0:T(8,128)}, f32[1536,512]{1,0:T(8,128)}, f32[1536,512]{1,0:T(8,128)}), (f32[1536,512]{1,0:T(8,128)}, f32[1536,512]{1,0:T(8,128)}, f32[1536,512]{1,0:T(8,128)}, ...) | async-done | bytes 12582928 | tf_op jit(solution)/shard_map/psum | solution.py:13
  316.4 34.6 %fusion.2 = f32[3072,1536]{1,0:T(8,128)} fusion(f32[1536,512]{1,0:T(8,128)S(1)} %copy-done.1, f32[1536,512]{1,0:T(8,128)} %get-tuple-element.16, f32[1536,512]{1,0:T(8,128)} %get-tuple-element.17), kind=kOutput, calls=%fused_computation.3 | convolution fusion | flops 28992602112 | bytes 28311552 | tf_op jit(solution)/shard_map/dot_general | solution.py:32
  351.0 39.2 %fusion.1 = f32[1536,3072]{0,1:T(8,128)S(1)} fusion(f32[1536,3072]{0,1:T(8,128)} %copy.11, f32[3072,1536]{1,0:T(8,128)} %fusion.2, f32[1536,512]{1,0:T(8,128)} %all-gather.21.cloned.1.call-done, f32[1536]{0:T(1024)S(1)} %copy-done.10, s32[1536]{0:T(1024)S(1)} %iota_add_fusion.1, s32[3072]{0:T(1024)S(1)} %iota_add_fusion, f32[1536,512]{1,0:T(8,128)} %get-tuple-element.18, ...), kind=kOutput, calls=%fused_computation.2 | convolution fusion | flops 29020913664 | bytes 66084864 | tf_op jit(solution)/shard_map/dot_general | solution.py:32
  390.2 6.5 copy-done
  396.7 19.5 %psum.39 = f32[1536,8]{0,1:T(8,128)S(1)} all-reduce(f32[1536,8]{0,1:T(8,128)S(1)} %slice_select_fusion), channel_id=1, replica_groups=mesh['row'=8,'col'=4] {'col'}, use_global_device_ids=true, to_apply=%region_4.5 | all-reduce | flops 12288 | bytes 98304 | tf_op jit(solution)/shard_map/psum | solution.py:13
  416.2 9.5 all_gather.59
  430.6 12.9 %fusion.16 = f32[1,1,12288]{2,1,0:T(1,128)S(1)} fusion(f32[1,1,12288]{2,1,0:T(1,128)S(1)} %broadcast.270.clone, s32[]{:T(128)S(6)} %select_n.118, f32[1536,3072]{0,1:T(8,128)} %copy-done, f32[3072,1]{0,1:T(1,128)S(1)} %bitcast.340), kind=kOutput, calls=%fused_computation.25 | convolution fusion | flops 56623104 | bytes 18892804 | tf_op jit(solution)/shard_map/dot_general | solution.py:68
  446.0 50.5 %all-gather.23.cloned.1.call-done = f32[32,1,12288]{2,1,0:T(1,128)} async-done(((f32[1,1,12288]{2,1,0:T(1,128)}), f32[32,1,12288]{2,1,0:T(1,128)}) %all-gather.23.cloned.1.call-update) | async-done | bytes 1572880 | tf_op jit(solution)/shard_map/all_gather | solution.py:72
  506.3 12.9 %fusion.15 = f32[1,1,12288]{2,1,0:T(1,128)S(1)} fusion(f32[1,1,12288]{2,1,0:T(1,128)S(1)} %broadcast.270.clone.1, s32[]{:T(128)S(6)} %select_n.118, f32[1536,3072]{0,1:T(8,128)} %copy-done, f32[3072,1]{0,1:T(1,128)S(1)} %bitcast.341), kind=kOutput, calls=%fused_computation.23 | convolution fusion | flops 56623104 | bytes 18892804 | tf_op jit(solution)/shard_map/dot_general | solution.py:68
  523.2 50.6 %all-gather.25.cloned.1.call-done = f32[32,1,12288]{2,1,0:T(1,128)} async-done(((f32[1,1,12288]{2,1,0:T(1,128)}), f32[32,1,12288]{2,1,0:T(1,128)}) %all-gather.25.cloned.1.call-update) | async-done | bytes 1572880 | tf_op jit(solution)/shard_map/all_gather | solution.py:72
  573.9 2.4 reduce_sum.220
  583.3 12.9 %fusion.14 = f32[1,1,12288]{2,1,0:T(1,128)S(1)} fusion(f32[1,1,12288]{2,1,0:T(1,128)S(1)} %broadcast.270.clone.2, s32[]{:T(128)S(6)} %select_n.118, f32[1536,3072]{0,1:T(8,128)} %copy-done, f32[3072,1]{0,1:T(1,128)S(1)} %bitcast.342), kind=kOutput, calls=%fused_computation.21 | convolution fusion | flops 56623104 | bytes 18892804 | tf_op jit(solution)/shard_map/dot_general | solution.py:68
  600.3 50.5 %all-gather.27.cloned.1.call-done = f32[32,1,12288]{2,1,0:T(1,128)} async-done(((f32[1,1,12288]{2,1,0:T(1,128)}), f32[32,1,12288]{2,1,0:T(1,128)}) %all-gather.27.cloned.1.call-update) | async-done | bytes 1572880 | tf_op jit(solution)/shard_map/all_gather | solution.py:72
  650.9 2.4 reduce_sum.223
  660.3 12.9 %fusion.13 = f32[1,1,12288]{2,1,0:T(1,128)S(1)} fusion(f32[1,1,12288]{2,1,0:T(1,128)S(1)} %broadcast.270.clone.3, s32[]{:T(128)S(6)} %select_n.118, f32[1536,3072]{0,1:T(8,128)} %copy-done, f32[3072,1]{0,1:T(1,128)S(1)} %bitcast.343), kind=kOutput, calls=%fused_computation.19 | convolution fusion | flops 56623104 | bytes 18892804 | tf_op jit(solution)/shard_map/dot_general | solution.py:68
  677.7 50.3 %all-gather.29.cloned.1.call-done = f32[32,1,12288]{2,1,0:T(1,128)} async-done(((f32[1,1,12288]{2,1,0:T(1,128)}), f32[32,1,12288]{2,1,0:T(1,128)}) %all-gather.29.cloned.1.call-update) | async-done | bytes 1572880 | tf_op jit(solution)/shard_map/all_gather | solution.py:72
  737.5 12.9 %fusion.12 = f32[1,1,12288]{2,1,0:T(1,128)S(1)} fusion(f32[1,1,12288]{2,1,0:T(1,128)S(1)} %broadcast.270.clone.4, s32[]{:T(128)S(6)} %select_n.118, f32[1536,3072]{0,1:T(8,128)} %copy-done, f32[3072,1]{0,1:T(1,128)S(1)} %bitcast.344), kind=kOutput, calls=%fused_computation.17 | convolution fusion | flops 56623104 | bytes 18892804 | tf_op jit(solution)/shard_map/dot_general | solution.py:68
  754.5 50.5 %all-gather.31.cloned.1.call-done = f32[32,1,12288]{2,1,0:T(1,128)} async-done(((f32[1,1,12288]{2,1,0:T(1,128)}), f32[32,1,12288]{2,1,0:T(1,128)}) %all-gather.31.cloned.1.call-update) | async-done | bytes 1572880 | tf_op jit(solution)/shard_map/all_gather | solution.py:72
  814.8 12.9 %fusion.11 = f32[1,1,12288]{2,1,0:T(1,128)S(1)} fusion(f32[1,1,12288]{2,1,0:T(1,128)S(1)} %broadcast.270.clone.5, s32[]{:T(128)S(6)} %select_n.118, f32[1536,3072]{0,1:T(8,128)} %copy-done, f32[3072,1]{0,1:T(1,128)S(1)} %bitcast.345), kind=kOutput, calls=%fused_computation.15 | convolution fusion | flops 56623104 | bytes 18892804 | tf_op jit(solution)/shard_map/dot_general | solution.py:68
  832.0 50.4 %all-gather.33.cloned.1.call-done = f32[32,1,12288]{2,1,0:T(1,128)} async-done(((f32[1,1,12288]{2,1,0:T(1,128)}), f32[32,1,12288]{2,1,0:T(1,128)}) %all-gather.33.cloned.1.call-update) | async-done | bytes 1572880 | tf_op jit(solution)/shard_map/all_gather | solution.py:72
  891.7 12.9 %fusion.10 = f32[1,1,12288]{2,1,0:T(1,128)S(1)} fusion(f32[1,1,12288]{2,1,0:T(1,128)S(1)} %broadcast.270.clone.6, s32[]{:T(128)S(6)} %select_n.118, f32[1536,3072]{0,1:T(8,128)} %copy-done, f32[3072,1]{0,1:T(1,128)S(1)} %bitcast.346), kind=kOutput, calls=%fused_computation.13 | convolution fusion | flops 56623104 | bytes 18892804 | tf_op jit(solution)/shard_map/dot_general | solution.py:68
  908.5 50.8 %all-gather.35.cloned.1.call-done = f32[32,1,12288]{2,1,0:T(1,128)} async-done(((f32[1,1,12288]{2,1,0:T(1,128)}), f32[32,1,12288]{2,1,0:T(1,128)}) %all-gather.35.cloned.1.call-update) | async-done | bytes 1572880 | tf_op jit(solution)/shard_map/all_gather | solution.py:72
  968.4 12.9 %fusion.9 = f32[1,1,12288]{2,1,0:T(1,128)S(1)} fusion(f32[1,1,12288]{2,1,0:T(1,128)S(1)} %broadcast.270, s32[]{:T(128)S(6)} %select_n.118, f32[1536,3072]{0,1:T(8,128)} %copy-done, f32[3072,1]{0,1:T(1,128)S(1)} %bitcast.339), kind=kOutput, calls=%fused_computation.11 | convolution fusion | flops 56623104 | bytes 18892804 | tf_op jit(solution)/shard_map/dot_general | solution.py:68
  981.9 18.7 %copy.12 = f32[1536,3072]{1,0:T(8,128)} copy(f32[1536,3072]{0,1:T(8,128)} %copy-done) | data formatting | bytes 37748736
  1000.7 5.0 stack.39
  1009.3 26.7 %all-gather.37.cloned.1.call-done = f32[32,1,12288]{2,1,0:T(1,128)} async-done(((f32[1,1,12288]{2,1,0:T(1,128)}), f32[32,1,12288]{2,1,0:T(1,128)}) %all-gather.37.cloned.1.call-update) | async-done | bytes 1572880 | tf_op jit(solution)/shard_map/all_gather | solution.py:72
  (188 shorter events, 82.3 us)
Async XLA Ops:
  7.2 69.2 %all-gather.21.cloned.1.call-start = ((), (), s32[]{:S(2)}) async-start(), calls=%async_computation.1 | async-start | bytes 3932160 | tf_op jit(solution)/shard_map/all_gather | solution.py:27
  9.9 130.1 %all-gather.19.cloned.1.call-start = ((), (), s32[]{:S(2)}) async-start(), calls=%async_computation | async-start | bytes 3932160 | tf_op jit(solution)/shard_map/all_gather | solution.py:27
  10.6 305.7 %all-reduce.3.cloned.1.call-start = ((), (), s32[]{:S(2)}) async-start(), calls=%async_computation.10 | async-start | bytes 25165824 | tf_op jit(solution)/shard_map/psum | solution.py:13
  145.6 350.9 %all-gather.23.cloned.1.call-start = ((), (), s32[]{:S(2)}) async-start(), calls=%async_computation.2 | async-start | bytes 1622016 | tf_op jit(solution)/shard_map/all_gather | solution.py:72
  146.3 170.1 %copy-start.1 = (f32[1536,512]{1,0:T(8,128)S(1)}, f32[1536,512]{1,0:T(8,128)}, u32[]{:S(2)}) copy-start(f32[1536,512]{1,0:T(8,128)} %all-gather.19.cloned.1.call-done) | copy-start | bytes 9437188
  316.4 34.6 %copy-start.10 = (f32[1536]{0:T(1024)S(1)}, f32[1536]{0:T(1024)}, u32[]{:S(2)}) copy-start(f32[1536]{0:T(1024)} %param.5) | copy-start | bytes 18436
  390.2 6.5 copy-start
  443.5 0.6 copy-start.2
  444.1 129.7 %all-gather.25.cloned.1.call-start = ((), (), s32[]{:S(2)}) async-start(), calls=%async_computation.3 | async-start | bytes 1622016 | tf_op jit(solution)/shard_map/all_gather | solution.py:72
  519.2 0.6 copy-start.3
  519.8 131.0 %all-gather.27.cloned.1.call-start = ((), (), s32[]{:S(2)}) async-start(), calls=%async_computation.4 | async-start | bytes 1622016 | tf_op jit(solution)/shard_map/all_gather | solution.py:72
  596.2 0.6 copy-start.4
  596.8 131.2 %all-gather.29.cloned.1.call-start = ((), (), s32[]{:S(2)}) async-start(), calls=%async_computation.5 | async-start | bytes 1622016 | tf_op jit(solution)/shard_map/all_gather | solution.py:72
  673.2 0.6 copy-start.5
  673.9 131.2 %all-gather.31.cloned.1.call-start = ((), (), s32[]{:S(2)}) async-start(), calls=%async_computation.6 | async-start | bytes 1622016 | tf_op jit(solution)/shard_map/all_gather | solution.py:72
  750.4 0.6 copy-start.6
  751.0 131.3 %all-gather.33.cloned.1.call-start = ((), (), s32[]{:S(2)}) async-start(), calls=%async_computation.7 | async-start | bytes 1622016 | tf_op jit(solution)/shard_map/all_gather | solution.py:72
  827.7 0.6 copy-start.7
  828.3 131.0 %all-gather.35.cloned.1.call-start = ((), (), s32[]{:S(2)}) async-start(), calls=%async_computation.8 | async-start | bytes 1622016 | tf_op jit(solution)/shard_map/all_gather | solution.py:72
  904.6 0.6 copy-start.8
  905.2 130.8 %all-gather.37.cloned.1.call-start = ((), (), s32[]{:S(2)}) async-start(), calls=%async_computation.9 | async-start | bytes 1622016 | tf_op jit(solution)/shard_map/all_gather | solution.py:72
  981.3 0.6 copy-start.9
Sparse Core Ops, SparseCore 0:
  10.1 66.1 all-gather.20
  77.9 62.0 all-gather.18
  145.7 170.6 all-reduce.2
  444.3 52.2 all-gather.22
  519.9 53.8 all-gather.24
  596.9 53.8 all-gather.26
  674.0 53.9 all-gather.28
  751.1 53.8 all-gather.30
  828.4 53.8 all-gather.32
  905.3 53.8 all-gather.34
  982.0 53.9 all-gather.36
